TPU v7x, 32 devices: a 4x4x1 block of a 4x4x8 slice. The times are simulated.
32 devices in a mesh: dp: 1 (over z), fsdp: 32 (over y, x, core).
Axes of the slice: x: 4, y: 4, z: 1, core: 2. Of those that a mesh axis runs over, the one named last changes fastest.
The devices are a block of a 4x4x8 slice.
Arguments:
- tokens: bfloat16 [256, 128, 7168], P(('dp', 'fsdp'))
- gain_in: bfloat16 [7168], P('fsdp')
- w_dq: bfloat16 [7168, 1536], P('fsdp')
- gain_q: bfloat16 [1536], P('fsdp')
- w_uq: bfloat16 [1536, 12288], P('fsdp')
- w_dkv: bfloat16 [7168, 576], P('fsdp')
- gain_kv: bfloat16 [512], P('fsdp')
- w_ukv: bfloat16 [512, 16384], P('fsdp')
- w_out: bfloat16 [8192, 7168], P('fsdp')
Outputs:
- output 1: bfloat16 [256, 128, 7168], P(('dp', 'fsdp'))
- output 2: bfloat16 [256, 128, 512], P(('dp', 'fsdp'))
- output 3: bfloat16 [256, 128, 64], P(('dp', 'fsdp'))
All inputs are finite; a program needn't handle non-finite values.
Results may differ from a plain program's by a relative error of at most 0.00639726.
Values are sent between devices in bfloat16 or wider.
A program may use at most 768 MiB of HBM per device.

v0:
```python
import jax
import jax.numpy as jnp
from jax import lax
from jax.sharding import PartitionSpec as P, NamedSharding

EPSILON = 1e-6
ROPE_THETA = 10000.0


def rms_scale(values_in, gain_vec):
    values_f32 = values_in.astype(jnp.float32)
    inv_rms = lax.rsqrt(jnp.mean(values_f32 * values_f32, axis=-1, keepdims=True) + EPSILON)
    return values_f32 * inv_rms * gain_vec.astype(jnp.float32)


def rope_tables(seq_len, rope_dim):
    half_dim = rope_dim // 2
    inv_freq = ROPE_THETA ** (-2.0 * jnp.arange(half_dim, dtype=jnp.float32) / rope_dim)
    angles = jnp.arange(seq_len, dtype=jnp.float32)[:, None] * inv_freq[None, :]
    return jnp.cos(angles), jnp.sin(angles)


def apply_rope(values_in, cos_t, sin_t):
    half_dim = values_in.shape[-1] // 2
    lo_half = values_in[..., :half_dim]
    hi_half = values_in[..., half_dim:]
    return jnp.concatenate([lo_half * cos_t - hi_half * sin_t, hi_half * cos_t + lo_half * sin_t], axis=-1)


def head_dims(w_uq, w_dkv, gain_kv, w_ukv, w_out):
    rope_dim = w_dkv.shape[1] - gain_kv.shape[0]
    nope_total = w_ukv.shape[1] - w_out.shape[0]
    n_heads = (w_uq.shape[1] - nope_total) // rope_dim
    return n_heads, nope_total // n_heads, rope_dim, w_out.shape[0] // n_heads


def latents(tokens, gain_in, w_dq, gain_q, w_dkv, gain_kv, cos_t, sin_t):
    kv_rank = gain_kv.shape[0]
    normed = rms_scale(tokens, gain_in).astype(jnp.bfloat16)
    q_down = jnp.einsum('btd,dr->btr', normed, w_dq, preferred_element_type=jnp.float32)
    q_lat = rms_scale(q_down, gain_q).astype(jnp.bfloat16)
    kv_down = jnp.einsum('btd,dr->btr', normed, w_dkv, preferred_element_type=jnp.float32)
    latent = rms_scale(kv_down[:, :, :kv_rank], gain_kv).astype(jnp.bfloat16)
    k_pe = apply_rope(kv_down[:, :, kv_rank:], cos_t, sin_t).astype(jnp.bfloat16)
    return q_lat, latent, k_pe


def attend(q_lat, latent, k_pe, w_uq, w_ukv, w_out, head_info, cos_t, sin_t):
    n_heads, nope_dim, rope_dim, v_dim = head_info
    n_prompts = q_lat.shape[0]
    seq_len = q_lat.shape[1]
    q_full = jnp.einsum('btr,rc->btc', q_lat, w_uq, preferred_element_type=jnp.float32)
    q_full = q_full.reshape(n_prompts, seq_len, n_heads, nope_dim + rope_dim)
    q_nope = q_full[..., :nope_dim].astype(jnp.bfloat16)
    q_pe = apply_rope(q_full[..., nope_dim:], cos_t[:, None, :], sin_t[:, None, :]).astype(jnp.bfloat16)
    kv_up = jnp.einsum('btr,rc->btc', latent, w_ukv, preferred_element_type=jnp.float32).astype(jnp.bfloat16)
    kv_up = kv_up.reshape(n_prompts, seq_len, n_heads, nope_dim + v_dim)
    k_nope = kv_up[..., :nope_dim]
    values = kv_up[..., nope_dim:]
    score_scale = (nope_dim + rope_dim) ** -0.5
    scores = jnp.einsum('bqhd,bkhd->bhqk', q_nope, k_nope, preferred_element_type=jnp.float32)
    scores = scores + jnp.einsum('crie,cle->cirl', q_pe, k_pe, preferred_element_type=jnp.float32)
    causal = jnp.arange(seq_len)[:, None] >= jnp.arange(seq_len)[None, :]
    scores = jnp.where(causal, scores * score_scale, -1e30)
    attn_probs = jax.nn.softmax(scores, axis=-1).astype(jnp.bfloat16)
    attn_out = jnp.einsum('bhqk,bkhd->bqhd', attn_probs, values, preferred_element_type=jnp.float32).astype(jnp.bfloat16)
    attn_out = attn_out.reshape(n_prompts, seq_len, n_heads * v_dim)
    return jnp.einsum('btc,cd->btd', attn_out, w_out, preferred_element_type=jnp.float32)


def solution(mesh):
    batch_spec = P(('dp', 'fsdp'))
    row_spec = P('fsdp')
    mat_spec = P('fsdp', None)

    def run_block(tokens, gain_in, w_dq, gain_q, w_uq, w_dkv, gain_kv, w_ukv, w_out):
        head_info = head_dims(w_uq, w_dkv, gain_kv, w_ukv, w_out)
        seq_len = tokens.shape[1]

        def local_block(tok_blk, gain_in_s, w_dq_s, gain_q_s, w_uq_s, w_dkv_s, gain_kv_s, w_ukv_s, w_out_s):
            cos_t, sin_t = rope_tables(seq_len, head_info[2])
            gain_in_all = lax.all_gather(gain_in_s, 'fsdp', tiled=True)
            w_dq_all = lax.all_gather(w_dq_s, 'fsdp', tiled=True)
            gain_q_all = lax.all_gather(gain_q_s, 'fsdp', tiled=True)
            w_dkv_all = lax.all_gather(w_dkv_s, 'fsdp', tiled=True)
            gain_kv_all = lax.all_gather(gain_kv_s, 'fsdp', tiled=True)
            q_lat, latent, k_pe = latents(tok_blk, gain_in_all, w_dq_all, gain_q_all, w_dkv_all, gain_kv_all, cos_t, sin_t)
            w_uq_all = lax.all_gather(w_uq_s, 'fsdp', tiled=True)
            w_ukv_all = lax.all_gather(w_ukv_s, 'fsdp', tiled=True)
            w_out_all = lax.all_gather(w_out_s, 'fsdp', tiled=True)
            proj_out = attend(q_lat, latent, k_pe, w_uq_all, w_ukv_all, w_out_all, head_info, cos_t, sin_t)
            y_blk = (tok_blk.astype(jnp.float32) + proj_out).astype(jnp.bfloat16)
            return y_blk, latent, k_pe

        mapped = jax.shard_map(
            local_block,
            mesh=mesh,
            in_specs=(batch_spec, row_spec, mat_spec, row_spec, mat_spec, mat_spec, row_spec, mat_spec, mat_spec),
            out_specs=(batch_spec, batch_spec, batch_spec),
            check_vma=False,
        )
        return mapped(tokens, gain_in, w_dq, gain_q, w_uq, w_dkv, gain_kv, w_ukv, w_out)

    return run_block
```

profile of v0, /device:TPU:97, one launch (start us, length us, event | category | flops | bytes accessed | tf_op | source)
XLA Modules:
  0.0 803.5 jit_solution(2425839669072223504)
XLA Ops:
  7.2 0.1 all-gather.6.cloned.1.call-start
  7.2 0.7 all-gather.6.cloned.1.call-update
  8.0 0.1 all-gather.8.cloned.1.call-start
  8.0 0.7 all-gather.8.cloned.1.call-update
  8.8 0.1 all-gather.10.cloned.1.call-start
  8.8 0.7 all-gather.10.cloned.1.call-update
  9.6 0.1 all-gather.12.cloned.1.call-start
  9.6 0.6 all-gather.12.cloned.1.call-update
  10.2 0.1 all-gather.14.cloned.1.call-start
  10.3 0.6 all-gather.14.cloned.1.call-update
  10.9 0.9 dynamic-update-slice
  11.7 0.8 dynamic-update-slice.2
  12.6 0.8 dynamic-update-slice.1
  13.4 51.4 %all-reduce.3 = (bf16[7168]{0:T(1024)(128)(2,1)S(1)}, bf16[1536]{0:T(1024)(128)(2,1)S(1)}, bf16[512]{0:T(512)(128)(2,1)S(1)}) all-reduce(bf16[7168]{0:T(1024)(128)(2,1)S(1)} %dynamic-update-slice, bf16[1536]{0:T(1024)(128)(2,1)S(1)} %dynamic-update-slice.2, bf16[512]{0:T(512)(128)(2,1)S(1)} %dynamic-update-slice.1), channel_id=1, replica_groups=mesh['dp'=1,'fsdp'=32] {'fsdp'}, use_global_device_ids=true, to_apply=%add | all-reduce | flops 9216 | bytes 36864
  64.8 0.6 iota_compare_fusion
  65.4 8.1 %fusion.7 = f32[8,128]{1,0:T(8,128)S(1)} fusion(bf16[8,128,7168]{2,1,0:T(8,128)(2,1)} %param.9), kind=kLoop, calls=%fused_computation.15 | loop fusion | flops 22019072 | bytes 14684160 | tf_op jit(solution)/shard_map/reduce_sum | solution.py:12
  73.5 0.1 fusion.38
  73.7 0.0 copy-start.2
  73.7 0.0 copy-start.4
  73.7 0.0 all-gather.6.cloned.1.call-done
  73.7 13.2 %fusion.24 = f32[8,128,576]{1,2,0:T(8,128)S(1)} fusion(bf16[8,128,7168]{2,1,0:T(8,128)(2,1)} %param.9, f32[7168]{0:T(1024)S(1)} %convert_element_type.41, f32[8,128]{1,0:T(8,128)S(1)} %add_rsqrt_fusion.2, bf16[7168,576]{1,0:T(8,128)(2,1)} %all-gather.6.cloned.1.call-done), kind=kOutput, calls=%fused_computation.27 | convolution fusion | flops 8485076992 | bytes 25329664 | tf_op jit(solution)/shard_map/btd,dr->btr/dot_general | solution.py:42
  86.9 0.1 multiply_reduce_fusion.1
  87.1 0.3 multiply_convert_fusion.2
  87.3 1.3 copy.36
  88.7 0.0 copy-done.2
  88.7 0.0 copy-done.4
  88.7 0.7 pad_maximum_fusion
  89.4 43.9 %all-gather.8.cloned.1.call-done = bf16[512,16384]{1,0:T(8,128)(2,1)} async-done(((bf16[16,16384]{1,0:T(8,128)(2,1)}), bf16[512,16384]{1,0:T(8,128)(2,1)}) %all-gather.8.cloned.1.call-update) | async-done | bytes 16777232 | tf_op jit(solution)/shard_map/all_gather | solution.py:89
  133.2 27.5 %convolution_convert_fusion = bf16[8,128,16384]{2,1,0:T(8,128)(2,1)} fusion(bf16[8,128,512]{1,2,0:T(8,128)(2,1)S(1)} %multiply_convert_fusion.2, bf16[512,16384]{1,0:T(8,128)(2,1)} %all-gather.8.cloned.1.call-done), kind=kOutput, calls=%fused_computation.14 | convolution fusion | flops 17196646400 | bytes 51380224 | tf_op jit(solution)/shard_map/btr,rc->btc/dot_general | solution.py:56
  160.7 23.0 %copy.45 = bf16[128,8,64,256]{3,2,1,0:T(8,128)(2,1)} copy(bf16[128,8,64,256]{3,1,2,0:T(8,128)(2,1)} %bitcast.46) | data formatting | bytes 67108864
  183.7 25.2 %fusion.40 = (bf16[8,128,64,128]{3,2,1,0:T(8,128)(2,1)}, bf16[8,128,64,128]{3,2,1,0:T(8,128)(2,1)}) fusion(bf16[8,128,64,256]{3,2,1,0:T(8,128)(2,1)} %bitcast.43), kind=kLoop, calls=%fused_computation.55 | loop fusion | bytes 67108864 | tf_op jit(solution)/shard_map/slice | solution.py:59
  208.9 5.2 all-gather.10.cloned.1.call-done
  214.2 30.6 %multiply_reduce_fusion = (f32[8,128]{1,0:T(8,128)S(1)}, f32[8,128,1536]{2,1,0:T(8,128)}) fusion(bf16[7168,1536]{1,0:T(8,128)(2,1)} %all-gather.10.cloned.1.call-done, bf16[8,128,7168]{2,1,0:T(8,128)(2,1)} %param.9, f32[7168]{0:T(1024)S(1)} %convert_element_type.41, f32[8,128]{1,0:T(8,128)S(1)} %add_rsqrt_fusion.2), kind=kOutput, calls=%fused_computation.37 | convolution fusion | flops 22581084160 | bytes 43028480 | tf_op jit(solution)/shard_map/btd,dr->btr/dot_general | solution.py:40
  244.8 90.2 %all-gather.12.cloned.1.call-done = bf16[1536,12288]{1,0:T(8,128)(2,1)} async-done(((bf16[48,12288]{1,0:T(8,128)(2,1)}), bf16[1536,12288]{1,0:T(8,128)(2,1)}) %all-gather.12.cloned.1.call-update) | async-done | bytes 37748752 | tf_op jit(solution)/shard_map/all_gather | solution.py:88
  334.9 0.0 copy-start.3
  334.9 0.0 copy-start.5
  334.9 49.8 %fusion.3 = f32[8,128,12288]{1,2,0:T(8,128)} fusion(bf16[1536,12288]{1,0:T(8,128)(2,1)} %all-gather.12.cloned.1.call-done, f32[8,128,1536]{2,1,0:T(8,128)} %get-tuple-element.24, f32[1536]{0:T(1024)S(1)} %convert_element_type.46, f32[8,128]{1,0:T(8,128)S(1)} %add_rsqrt_fusion), kind=kOutput, calls=%fused_computation.6 | convolution fusion | flops 38659424256 | bytes 94382080 | tf_op jit(solution)/shard_map/btr,rc->btc/dot_general | solution.py:52
  384.7 0.0 copy-start.1
  384.7 0.0 copy-done.3
  384.7 0.0 copy-done.5
  384.7 9.2 %subtract_convert_fusion = (bf16[8,128,64,32]{1,3,2,0:T(8,128)(2,1)S(1)}, bf16[8,128,64,32]{1,3,2,0:T(8,128)(2,1)}) fusion(f32[8,128,64,192]{1,3,2,0:T(8,128)} %bitcast.44, f32[128,32]{0,1:T(8,128)S(1)} %copy-done.5, f32[128,32]{0,1:T(8,128)S(1)} %copy-done.3), kind=kLoop, calls=%fused_computation.35 | loop fusion | flops 16777216 | bytes 25198592 | tf_op jit(solution)/shard_map/convert | solution.py:102
  393.9 0.0 copy-done.1
  393.9 14.8 %fusion.30 = f32[8,128,128,64]{2,1,3,0:T(8,128)} fusion(bf16[8,128,64,32]{1,3,2,0:T(8,128)(2,1)} %get-tuple-element.16, bf16[8,128,64,32]{1,3,2,0:T(8,128)(2,1)S(1)} %get-tuple-element.15, bf16[8,128,64]{1,2,0:T(8,128)(2,1)S(1)} %copy-done.1), kind=kOutput, calls=%fused_computation.30 | convolution fusion | flops 1090519040 | bytes 42074112 | tf_op jit(solution)/shard_map/crie,cle->cirl/dot_general | solution.py:62
  408.7 0.0 copy-done
  408.7 44.0 %fusion.41 = (f32[8,64,128]{2,1,0:T(8,128)S(1)}, f32[8,64,128,128]{2,3,1,0:T(8,128)}) fusion(f32[8,128,128,64]{2,1,3,0:T(8,128)} %fusion.30, pred[128,128]{0,1:T(8,128)(4,1)S(1)} %copy-done, f32[8,128,64,192]{1,3,2,0:T(8,128)} %bitcast.45, bf16[8,128,64,128]{3,2,1,0:T(8,128)(2,1)} %get-tuple-element.18), kind=kOutput, calls=%fused_computation.56 | convolution fusion | flops 2189426688 | bytes 100941824 | tf_op jit(solution)/shard_map/sub | solution.py:65
  452.7 24.8 %fusion.26 = bf16[8,64,128,128]{3,2,1,0:T(8,128)(2,1)} fusion(f32[8,64,128,128]{2,3,1,0:T(8,128)} %get-tuple-element.26, f32[8,64,128]{2,1,0:T(8,128)S(1)} %get-tuple-element.25, bf16[8,128,64,128]{3,2,1,0:T(8,128)(2,1)} %get-tuple-element.17), kind=kOutput, calls=%fused_computation.28 | convolution fusion | flops 2172649472 | bytes 67371008 | tf_op jit(solution)/shard_map/bhqk,bkhd->bqhd/dot_general | solution.py:66
  477.5 185.4 %all-gather.14.cloned.1.call-done = bf16[8192,7168]{1,0:T(8,128)(2,1)} async-done(((bf16[256,7168]{1,0:T(8,128)(2,1)}), bf16[8192,7168]{1,0:T(8,128)(2,1)}) %all-gather.14.cloned.1.call-update) | async-done | bytes 117440528 | tf_op jit(solution)/shard_map/all_gather | solution.py:90
  662.9 133.6 %fusion.10 = bf16[8,128,7168]{2,1,0:T(8,128)(2,1)} fusion(bf16[8,128,7168]{2,1,0:T(8,128)(2,1)} %param.9, bf16[8,128,8192]{1,2,0:T(8,128)(2,1)} %bitcast.47, bf16[8192,7168]{1,0:T(8,128)(2,1)} %all-gather.14.cloned.1.call-done), kind=kOutput, calls=%fused_computation.18 | convolution fusion | flops 120281104384 | bytes 163577856 | tf_op jit(solution)/shard_map/btc,cd->btd/dot_general | solution.py:68
  (12 shorter events, 0.1 us)
Async XLA Ops:
  7.2 66.5 %all-gather.6.cloned.1.call-start = ((), (), s32[]{:S(2)}) async-start(), calls=%async_computation | async-start | bytes 9461760 | tf_op jit(solution)/shard_map/all_gather | solution.py:85
  8.0 125.3 %all-gather.8.cloned.1.call-start = ((), (), s32[]{:S(2)}) async-start(), calls=%async_computation.1 | async-start | bytes 17301504 | tf_op jit(solution)/shard_map/all_gather | solution.py:89
  8.8 205.4 %all-gather.10.cloned.1.call-start = ((), (), s32[]{:S(2)}) async-start(), calls=%async_computation.2 | async-start | bytes 22708224 | tf_op jit(solution)/shard_map/all_gather | solution.py:83
  9.6 325.4 %all-gather.12.cloned.1.call-start = ((), (), s32[]{:S(2)}) async-start(), calls=%async_computation.3 | async-start | bytes 38928384 | tf_op jit(solution)/shard_map/all_gather | solution.py:88
  10.2 652.7 %all-gather.14.cloned.1.call-start = ((), (), s32[]{:S(2)}) async-start(), calls=%async_computation.4 | async-start | bytes 121110528 | tf_op jit(solution)/shard_map/all_gather | solution.py:90
  73.7 15.0 %copy-start.2 = (f32[128,32]{0,1:T(8,128)}, f32[128,32]{0,1:T(8,128)S(1)}, u32[]{:S(2)}) copy-start(f32[128,32]{0,1:T(8,128)S(1)} %get-tuple-element.21) | copy-start | bytes 49156
  73.7 15.0 %copy-start.4 = (f32[128,32]{0,1:T(8,128)}, f32[128,32]{0,1:T(8,128)S(1)}, u32[]{:S(2)}) copy-start(f32[128,32]{0,1:T(8,128)S(1)} %get-tuple-element.22) | copy-start | bytes 49156
  334.9 49.8 %copy-start.3 = (f32[128,32]{0,1:T(8,128)S(1)}, f32[128,32]{0,1:T(8,128)}, u32[]{:S(2)}) copy-start(f32[128,32]{0,1:T(8,128)} %copy-done.2) | copy-start | bytes 49156
  334.9 49.8 %copy-start.5 = (f32[128,32]{0,1:T(8,128)S(1)}, f32[128,32]{0,1:T(8,128)}, u32[]{:S(2)}) copy-start(f32[128,32]{0,1:T(8,128)} %copy-done.4) | copy-start | bytes 49156
  384.7 9.2 %copy-start.1 = (bf16[8,128,64]{1,2,0:T(8,128)(2,1)S(1)}, bf16[8,128,64]{1,2,0:T(8,128)(2,1)}, u32[]{:S(2)}) copy-start(bf16[8,128,64]{1,2,0:T(8,128)(2,1)} %pad_maximum_fusion) | copy-start | bytes 393220
  393.9 14.8 %copy-start = (pred[128,128]{0,1:T(8,128)(4,1)S(1)}, pred[128,128]{0,1:T(8,128)(4,1)}, u32[]{:S(2)}) copy-start(pred[128,128]{0,1:T(8,128)(4,1)} %iota_compare_fusion) | copy-start | bytes 49156
Sparse Core Ops, SparseCore 0:
  10.1 54.2 all-gather.5
  66.4 66.7 all-gather.7
  135.3 78.8 all-gather.9
  216.1 118.8 all-gather.11
  336.9 326.0 all-gather.13
where the time goes:
time: 811 us; the launch traced here: 804 us
  matrix products  338 us (42%)
  waiting for transfers between devices  328 us (40%)
  local copies, waits for them, and re-layouts  52.1 us (6%)
  blocking collectives  51.4 us (6%)
  other arithmetic  19.2 us (2%)
  between operations  14.4 us (2%)
    all_gather x1, waiting for transfers between devices, local_block(): w_out_all = lax.all_gather(w_out_s, 'fsdp', tiled=True)  185 us
    dot_general x1, matrix products, attend(): jnp.einsum('btc,cd->btd', attn_out, w_out, preferred_element_type=jnp.flo...  134 us
    all_gather x1, waiting for transfers between devices, local_block(): w_uq_all = lax.all_gather(w_uq_s, 'fsdp', tiled=True)  90.2 us
    unnamed x1, blocking collectives  51.4 us
    dot_general x1, matrix products, attend(): jnp.einsum('btr,rc->btc', q_lat, w_uq, preferred_element_type=jnp.float32)  49.8 us
    sub x1, matrix products, attend(): attn_probs = jax.nn.softmax(scores, axis=-1).astype(jnp.bfloat16)  44 us
    all_gather x1, waiting for transfers between devices, local_block(): w_ukv_all = lax.all_gather(w_ukv_s, 'fsdp', tiled=True)  43.9 us
    dot_general x1, matrix products, latents(): jnp.einsum('btd,dr->btr', normed, w_dq, preferred_element_type=jnp.float32)  30.6 us
  transfers between devices with their start and end apart: 5, of which 4 were waited for; matrix products, arithmetic and copies ran while one was open for 34% of the time, Pallas kernels for 0%

commit v1 on v0

v1 whole, which is shorter than its diff:
```python
import math

import jax
import jax.numpy as jnp
import numpy as np
from jax import lax
from jax.experimental import pallas as pl
from jax.experimental.pallas import tpu as pltpu
from jax.sharding import PartitionSpec as P

EPSILON = 1e-6
ROPE_THETA = 10000.0
NEG = -1e30
MESH = pl.DeviceIdType.MESH
F32 = jnp.float32
BF16 = jnp.bfloat16
LANES = 128
CORES = 2
GROUP_HEADS = 8
HALF = 4
WIDE = 512
NARROW = 256
ROWS = 256
HROWS = 512


def rope_tables(seq_len, rope_dim):
    half = rope_dim // 2
    inv_freq = ROPE_THETA ** (-2.0 * np.arange(half) / rope_dim)
    angles = np.arange(seq_len)[:, None] * inv_freq[None, :]
    cos, sin, zero = np.cos(angles), np.sin(angles), np.zeros_like(angles)
    reps = LANES // rope_dim
    c = np.tile(np.concatenate([cos, cos], 1), (1, reps))
    lo = np.tile(np.concatenate([-sin, zero], 1), (1, reps))
    hi = np.tile(np.concatenate([zero, sin], 1), (1, reps))
    return [t.astype(np.float32) for t in (c, lo, hi)]


def inv_rms(v, n):
    return lax.rsqrt(jnp.sum(v * v, axis=-1, keepdims=True) * (1.0 / n) + EPSILON)


class Chunk:
    def __init__(self, cid, kind, own, full, rows, col, width):
        self.cid, self.kind, self.own, self.full = cid, kind, own, full
        self.rows, self.cols = rows, pl.ds(col, width)


def make_kernel(n_dev, dims):
    side = math.isqrt(n_dev // CORES)
    (T, D, QR, KVR, H, NOPE, RD, VD, SEQ) = dims
    GW = GROUP_HEADS * (NOPE + RD)
    KVW = GROUP_HEADS * (NOPE + VD)
    n_groups = H // GROUP_HEADS
    r_d, r_q, r_kv, r_o = D // n_dev, QR // n_dev, KVR // n_dev, H * VD // n_dev
    scale = (NOPE + RD) ** -0.5
    half = RD // 2
    n_wide = D // (2 * WIDE) - 1

    def kernel(x, gp, wdkv, wdq, wuq, wukv, wo, tc, tlo, thi, cmask, lmask,
               y, lat, kpe, g_gp, g_dkv, g_dq, g_uq, g_ukv, g_o,
               act, cq, cl, rr, qdown, wbuf, xst, wq, wkv, qn, qp, kv, ys, gv,
               st_gp, st_dkv, st_dq, st_uq, st_ukv,
               send, recv, loc, stg, wsem, psem, xsem, ysem):
        me = lax.axis_index("fsdp")
        core = lax.rem(me, CORES)
        px = lax.rem(me // CORES, side)
        py = me // (CORES * side)
        up = lambda v, d: lax.rem(v + d, side)
        dev = lambda yy, xx, kk: {"fsdp": (yy * side + xx) * CORES + kk}
        partner = dev(py, px, 1 - core)

        barrier = pltpu.get_barrier_semaphore()
        near = [dev(py, up(px, 1), core), dev(py, up(px, side - 1), core),
                dev(up(py, 1), px, core), dev(up(py, side - 1), px, core), partner]
        for d in near:
            pl.semaphore_signal(barrier, inc=1, device_id=d, device_id_type=MESH)

        n_o = wo.shape[1] // WIDE
        stage_in, stage_out = [], []
        moves = [(gp, st_gp, g_gp), (wdkv, st_dkv, g_dkv), (wdq, st_dq, g_dq),
                 (wuq, st_uq, g_uq), (wukv, st_ukv, g_ukv)]
        for i, (own, st, full) in enumerate(moves):
            stage_in.append(pltpu.make_async_copy(own, st, stg.at[0, i]))
            stage_out.append(pltpu.make_async_copy(st, full.at[py, px, core], stg.at[1, i]))
        for j in range(n_o):
            c = pl.ds(j * WIDE, WIDE)
            stage_in.append(pltpu.make_async_copy(wo.at[:, c], wbuf.at[0, j], stg.at[0, len(moves) + j]))
            stage_out.append(pltpu.make_async_copy(wbuf.at[0, j], g_o.at[py, px, core, :, c], stg.at[1, len(moves) + j]))
        for c in stage_in:
            c.start()
        pl.semaphore_wait(barrier, len(near))

        rounds = [[("A", gp, g_gp, 16, 0, gp.shape[1]), ("A", wdkv, g_dkv, r_d, 0, wdkv.shape[1]),
                   ("B", wdq, g_dq, r_d, 0, WIDE)],
                  [("A", wdq, g_dq, r_d, WIDE, WIDE), ("B", wdq, g_dq, r_d, 2 * WIDE, WIDE)]]
        for g in range(0, n_groups, 2):
            rounds.append([("A", wuq, g_uq, r_q, g * GW, GW), ("A", wukv, g_ukv, r_kv, g * KVW, KVW),
                           ("B", wuq, g_uq, r_q, (g + 1) * GW, GW), ("B", wukv, g_ukv, r_kv, (g + 1) * KVW, KVW)])
        first_o = len(rounds)
        cid, fixed = 0, []
        for r in rounds:
            fixed.append([Chunk(cid + i, *c) for i, c in enumerate(r)])
            cid += len(r)
        last_wide = first_o + n_wide
        n_rounds = last_wide + 2

        def span_o(t, i, wide):
            if wide:
                return pl.multiple_of(((t - first_o) * 2 + i) * WIDE, WIDE), WIDE
            return pl.multiple_of(n_wide * 2 * WIDE + ((t - last_wide) * 2 + i) * NARROW, NARROW), NARROW

        def chunks(t, wide):
            if isinstance(t, int) and t < first_o:
                return fixed[t]
            return [Chunk(cid + (t - first_o) * 2 + i, k, wo, g_o, r_o, *span_o(t, i, wide)) for i, k in enumerate("AB")]

        def in_round(t, fn):
            if isinstance(t, int):
                if 0 <= t < n_rounds:
                    fn(t < last_wide)
            else:
                pl.when(t < last_wide)(lambda: fn(True))

                @pl.when(t >= last_wide)
                def _():
                    pl.when(t < n_rounds)(lambda: fn(False))

        every = slice(None)

        def copy_of(c, j):
            f, s = (px, py) if c.kind == "A" else (py, px)
            h = c.rows // 2
            top, bot = pl.ds(0, h), pl.ds(h, h)

            def block(b, a, rows=every):
                yy, xx = (b, a) if c.kind == "A" else (a, b)
                return c.full.at[yy, xx, core, rows, c.cols]

            def near_by(b, a):
                yy, xx = (b, a) if c.kind == "A" else (a, b)
                return dev(yy, xx, core)

            back = side - 1
            src = None
            if j == 0:
                src, dst, to = c.own.at[:, c.cols], block(s, f), near_by(s, up(f, 1))
            elif j == 1:
                src, dst, to = c.own.at[:, c.cols], block(s, f), near_by(s, up(f, back))
            elif j == 2:
                dst, to = block(s, up(f, back), top), near_by(s, up(f, 1))
            elif j == 3:
                dst, to = block(s, up(f, 1), bot), near_by(s, up(f, back))
            elif j == 4:
                dst, to = block(s, every), near_by(up(s, 1), f)
            elif j == 5:
                dst, to = block(s, every), near_by(up(s, back), f)
            elif j == 6:
                dst, to = block(up(s, back), every, top), near_by(up(s, 1), f)
            elif j == 7:
                dst, to = block(up(s, 1), every, bot), near_by(up(s, back), f)
            else:
                dst, to = block(up(s, (0, back, 1, 2)[j - 8]), every), partner
            return pltpu.make_async_remote_copy(src_ref=dst if src is None else src, dst_ref=dst,
                                                send_sem=send.at[c.cid, j], recv_sem=recv.at[c.cid, j],
                                                device_id=to, device_id_type=MESH)

        def steps(c, names):
            for n in names:
                if n < 0:
                    copy_of(c, ~n).wait_recv()
                else:
                    copy_of(c, n).start()

        S1, S2, S3 = (0, 1), (~0, 2, ~1, 3), (~2, ~3, 4, 5, 8)
        S4, S5, S6 = (~4, 6, 9, ~5, 7, 10), (~6, ~7, 11), (~8, ~9, ~10, ~11)

        def comm(t, names):
            def run(wide):
                for c in chunks(t, wide):
                    steps(c, names)
            in_round(t, run)

        def rows_of(m, n):
            return pl.ds(pl.multiple_of(m * n, n), n)

        def rope(v):
            return v * tc[...] + pltpu.roll(v, LANES - half, 1) * tlo[...] + pltpu.roll(v, half, 1) * thi[...]

        def gain_rows(row, count):
            part = count // n_dev
            width = math.lcm(part, LANES)
            period = width // part
            out = []
            for g in range(n_dev // period):
                tot = None
                for j in range(period):
                    i = g * period + j
                    v = gv[i // (side * CORES), (i // CORES) % side, i % CORES, :, :width].astype(F32)
                    tot = v if tot is None else tot + v
                out.append(tot[row:row + 1, :])
            return out, width

        def norm_tokens():
            cp = pltpu.make_async_copy(g_gp, gv, loc.at[0])
            cp.start()
            xrows = xst.shape[1]
            n = T // xrows
            load = lambda i, slot: pltpu.make_async_copy(x.at[rows_of(i, xrows), :], xst.at[slot], xsem.at[slot])
            load(0, 0).start()
            cp.wait()
            gains, width = gain_rows(0, D)

            @pl.loop(0, n, step=2)
            def _(i0):
                for slot in range(2):
                    i = i0 + slot
                    if slot == 0:
                        load(i + 1, 1).start()
                    else:
                        @pl.when(i + 1 < n)
                        def _():
                            load(i + 1, 0).start()
                    load(i, slot).wait()
                    ss = jnp.zeros((xrows, 1), F32)
                    for g in range(len(gains)):
                        v = xst[slot, :, g * width:(g + 1) * width].astype(F32)
                        ss = ss + jnp.sum(v * v, axis=-1, keepdims=True)
                    inv = lax.rsqrt(ss * (1.0 / D) + EPSILON)
                    for g in range(len(gains)):
                        v = xst[slot, :, g * width:(g + 1) * width].astype(F32)
                        act[rows_of(i, xrows), g * width:(g + 1) * width] = (v * inv * gains[g]).astype(BF16)

        def fetch_d(full, rows, col, width, slot):
            cps = []
            for yy in range(side):
                for xx in range(side):
                    i = (yy * side + xx) * CORES
                    cps.append(pltpu.make_async_copy(full.at[yy, xx, :, :, pl.ds(col, width)],
                                                     wbuf.at[slot, pl.ds(i, CORES), pl.ds(0, rows), pl.ds(0, width)],
                                                     wsem.at[slot, yy * side + xx]))
            return cps

        def start(cps):
            for c in cps:
                c.start()

        def wait(cps):
            for c in cps:
                c.wait()

        def kv_down():
            cps = fetch_d(g_dkv, r_d, 0, KVR, 0) + fetch_d(g_dkv, r_d, KVR, LANES, 1)
            start(cps)
            wait(cps)
            gains, width = gain_rows(2, KVR)
            gain = jnp.concatenate(gains, axis=1)

            @pl.loop(0, T // ROWS)
            def _(m):
                r = rows_of(m, ROWS)
                u = jnp.dot(act[r, :D], wbuf[0, :, :r_d, :].reshape(D, WIDE), preferred_element_type=F32)
                cl[r, :] = (u * inv_rms(u, KVR) * gain).astype(BF16)
                v = jnp.dot(act[r, :D], wbuf[1, :, :r_d, :LANES].reshape(D, LANES), preferred_element_type=F32)
                for b in range(ROWS // SEQ):
                    rr[pl.ds(pl.multiple_of(m * ROWS + b * SEQ, SEQ), SEQ), :] = rope(v[b * SEQ:(b + 1) * SEQ]).astype(BF16)
            pltpu.make_async_copy(cl, lat, loc.at[1]).start()
            pltpu.make_async_copy(rr, kpe, loc.at[2]).start()

        def q_down(j):
            slot = j % 2
            wait(fetch_d(g_dq, r_d, j * WIDE, WIDE, slot))

            @pl.loop(0, T // ROWS)
            def _(m):
                r = rows_of(m, ROWS)
                qdown[r, j * WIDE:(j + 1) * WIDE] = jnp.dot(act[r, :D], wbuf[slot, :, :r_d, :].reshape(D, WIDE),
                                                           preferred_element_type=F32)
            if j == QR // WIDE - 1:
                gains, width = gain_rows(1, QR)

                @pl.loop(0, T // LANES)
                def _(m):
                    r = rows_of(m, LANES)
                    inv = inv_rms(qdown[r, :], QR)
                    for g in range(len(gains)):
                        c = slice(g * width, (g + 1) * width)
                        cq[r, c] = (qdown[r, c] * inv * gains[g]).astype(BF16)

        def fetch_u(i):
            slot = lax.rem(i, 2)
            wa, wb = HALF * (NOPE + RD), HALF * (NOPE + VD)
            ca, cb = pl.ds(pl.multiple_of(i * wa, wa), wa), pl.ds(pl.multiple_of(i * wb, wb), wb)
            return [pltpu.make_async_copy(g_uq.at[:, :, :, :, ca], wq.at[slot], psem.at[0, slot]),
                    pltpu.make_async_copy(g_ukv.at[:, :, :, :, cb], wkv.at[slot], psem.at[1, slot])]

        def heads(i, more):
            slot = lax.rem(i, 2)

            @pl.when(more)
            def _():
                start(fetch_u(i + 1))
            wait(fetch_u(i))
            lo = lmask[0].astype(F32) > 0.5
            pw = 2 * (NOPE + RD)

            @pl.loop(0, T // HROWS)
            def _(m):
                c = cq[rows_of(m, HROWS), :]
                for p in range(HALF // 2):
                    v = jnp.dot(c, wq[slot, :, :, :, :, p * pw:(p + 1) * pw].reshape(QR, pw), preferred_element_type=F32)
                    v0, v1, v2 = (v[:, k * LANES:(k + 1) * LANES] for k in range(3))
                    qn[:, (2 * p) * NOPE:(2 * p + 1) * NOPE] = v0.astype(BF16)
                    qn[:, (2 * p + 1) * NOPE:(2 * p + 2) * NOPE] = pltpu.roll(jnp.where(lo, v2, v1), RD, 1).astype(BF16)
                    pe = jnp.where(lo, v1, v2)
                    for b in range(HROWS // SEQ):
                        rb = slice(b * SEQ, (b + 1) * SEQ)
                        qp[rb, p * LANES:(p + 1) * LANES] = rope(pe[rb]).astype(BF16)
                kv[...] = jnp.dot(cl[rows_of(m, HROWS), :], wkv[slot].reshape(KVR, HALF * (NOPE + VD)),
                                  preferred_element_type=F32).astype(BF16)
                units = [(b, h) for b in range(HROWS // SEQ) for h in range(HALF)]
                visible = cmask[...] > 0.5
                prompt = lambda b: pl.ds(pl.multiple_of(m * HROWS + b * SEQ, SEQ), SEQ)

                def score(b, h):
                    rb = slice(b * SEQ, (b + 1) * SEQ)
                    k0 = h * (NOPE + VD)
                    q_cat = jnp.concatenate([qn[rb, h * NOPE:(h + 1) * NOPE],
                                             qp[rb, (h // 2) * LANES:(h // 2 + 1) * LANES]], axis=1)
                    k_cat = jnp.concatenate([kv[rb, k0:k0 + NOPE], rr[prompt(b), :] * lmask[h % 2]], axis=1)
                    return lax.dot_general(q_cat, k_cat, (((1,), (1,)), ((), ())), preferred_element_type=F32)

                ss = [jnp.where(visible, score(b, h) * scale, NEG) for b, h in units]
                es = [jnp.exp(v - jnp.max(v, axis=-1, keepdims=True)) for v in ss]
                ps = [(e * (1.0 / jnp.sum(e, axis=-1, keepdims=True))).astype(BF16) for e in es]
                for pr, (b, h) in zip(ps, units):
                    v0 = h * (NOPE + VD) + NOPE
                    o = jnp.dot(pr, kv[b * SEQ:(b + 1) * SEQ, v0:v0 + VD], preferred_element_type=F32)
                    act[prompt(b), pl.ds(pl.multiple_of((i * HALF + h) * VD, VD), VD)] = o.astype(BF16)

        def fetch_o(t, i, wide):
            col, width = span_o(t, i, wide)
            return fetch_d(g_o, r_o, col, width, i) + [
                pltpu.make_async_copy(x.at[:, pl.ds(col, width)], ys.at[i, :, pl.ds(0, width)], xsem.at[i])]

        def put_o(t, i, wide):
            col, width = span_o(t, i, wide)
            return pltpu.make_async_copy(ys.at[i, :, pl.ds(0, width)], y.at[:, pl.ds(col, width)], ysem.at[i])

        def project(t, i):
            in_round(t, lambda wide: wait(fetch_o(t, i, wide)))

            @pl.loop(0, WIDE // NARROW - lax.div(t - first_o, n_wide))
            def _(n):
                c = pl.ds(pl.multiple_of(n * NARROW, NARROW), NARROW)

                @pl.loop(0, T // ROWS)
                def _(m):
                    r = rows_of(m, ROWS)
                    acc = jnp.dot(act[r, :], wbuf[i, :, :, c].reshape(H * VD, NARROW), preferred_element_type=F32)
                    ys[i, r, c] = (ys[i, r, c].astype(F32) + acc).astype(BF16)
            in_round(t, lambda wide: put_o(t, i, wide).start())

        def piece(t, i):
            if not isinstance(t, int):
                if i < 2:
                    project(t, i)
            elif t == 0:
                if i == 0:
                    norm_tokens()
                elif i == 1:
                    kv_down()
                    start(fetch_d(g_dq, r_d, 0, WIDE, 0))
                else:
                    q_down(0)
                    start(fetch_d(g_dq, r_d, 2 * WIDE, WIDE, 0))
            elif t == 1 and i < 2:
                q_down(1 + i)
            elif 2 <= t < first_o and i < 2:
                k0 = (t - 2) * 4 + i * 2
                pl.loop(k0, k0 + 2)(lambda k: heads(k, k < (t - 2) * 4 + 3))

        def prefetch(t):
            if not isinstance(t, int):
                for i in range(2):
                    @pl.when(t > first_o)
                    def _():
                        in_round(t - 1, lambda wide: put_o(t - 1, i, wide).wait())
                    in_round(t, lambda wide: start(fetch_o(t, i, wide)))
            elif t == 1:
                start(fetch_d(g_dq, r_d, WIDE, WIDE, 1))
            elif 2 <= t < first_o:
                start(fetch_u((t - 2) * 4))
            elif t == first_o:
                for i in range(2):
                    start(fetch_o(t, i, True))

        def tick(t):
            comm(t + 1, S1)
            comm(t, S2)
            piece(t - 2, 0)
            comm(t - 1, S4)
            comm(t, S3)
            piece(t - 2, 1)
            comm(t - 1, S5)
            comm(t - 1, S6)
            prefetch(t - 1)
            piece(t - 2, 2)

        comm(0, S1)
        wait(stage_in)
        start(stage_out)
        wait(stage_out)
        for t in range(first_o + 2):
            tick(t)
        pl.loop(first_o + 2, n_rounds + 2)(tick)

        pltpu.make_async_copy(cl, lat, loc.at[1]).wait()
        pltpu.make_async_copy(rr, kpe, loc.at[2]).wait()
        for r in fixed:
            for c in r:
                for j in range(12):
                    copy_of(c, j).wait_send()

        for lo, hi, wide in ((first_o, last_wide, True), (last_wide, n_rounds, False)):
            @pl.loop(lo, hi)
            def _(t):
                for c in chunks(t, wide):
                    for j in range(12):
                        copy_of(c, j).wait_send()

    n_chunks = 5 + 2 * n_groups + 2 * (n_wide + 2)
    gathered = lambda r, c: jax.ShapeDtypeStruct((side, side, CORES, r, c), BF16)
    lanes_gp = math.lcm(r_d, LANES)
    out_shape = [jax.ShapeDtypeStruct((T, D), BF16), jax.ShapeDtypeStruct((T, KVR), BF16),
                 jax.ShapeDtypeStruct((T, LANES), BF16), gathered(16, lanes_gp), gathered(r_d, KVR + LANES),
                 gathered(r_d, QR), gathered(r_q, n_groups * GW), gathered(r_kv, n_groups * KVW), gathered(r_o, D)]
    scratch = [pltpu.VMEM((T, H * VD), BF16), pltpu.VMEM((T, QR), BF16), pltpu.VMEM((T, KVR), BF16),
               pltpu.VMEM((T, LANES), BF16), pltpu.VMEM((T, QR), F32), pltpu.VMEM((2, n_dev, r_o, WIDE), BF16),
               pltpu.VMEM((2, 64, D), BF16),
               pltpu.VMEM((2, side, side, CORES, r_q, HALF * (NOPE + RD)), BF16),
               pltpu.VMEM((2, side, side, CORES, r_kv, HALF * (NOPE + VD)), BF16),
               pltpu.VMEM((HROWS, HALF * NOPE), BF16), pltpu.VMEM((HROWS, HALF * RD), BF16),
               pltpu.VMEM((HROWS, HALF * (NOPE + VD)), BF16), pltpu.VMEM((2, T, WIDE), BF16),
               pltpu.VMEM((side, side, CORES, 16, lanes_gp), BF16),
               pltpu.VMEM((16, lanes_gp), BF16), pltpu.VMEM((r_d, KVR + LANES), BF16), pltpu.VMEM((r_d, QR), BF16),
               pltpu.VMEM((r_q, n_groups * GW), BF16), pltpu.VMEM((r_kv, n_groups * KVW), BF16),
               pltpu.SemaphoreType.DMA((n_chunks, 12)), pltpu.SemaphoreType.DMA((n_chunks, 12)),
               pltpu.SemaphoreType.DMA((3,)), pltpu.SemaphoreType.DMA((2, 5 + D // WIDE)),
               pltpu.SemaphoreType.DMA((2, side * side)), pltpu.SemaphoreType.DMA((2, 2)),
               pltpu.SemaphoreType.DMA((2,)), pltpu.SemaphoreType.DMA((2,))]
    return kernel, out_shape, scratch


def hand_over(y_ref, lat_ref, kpe_ref, y_out, lat_out, kpe_out):
    y_out[...] = y_ref[...]
    lat_out[...] = lat_ref[...]
    kpe_out[...] = kpe_ref[:, :kpe_out.shape[1]]


def solution(mesh):
    batch_spec = P(('dp', 'fsdp'))
    row_spec = P('fsdp')
    mat_spec = P('fsdp', None)
    n_dev = mesh.shape['fsdp']

    def run_block(tokens, gain_in, w_dq, gain_q, w_uq, w_dkv, gain_kv, w_ukv, w_out):
        D, QR = w_dq.shape
        KVR = gain_kv.shape[0]
        RD = w_dkv.shape[1] - KVR
        nope_total = w_ukv.shape[1] - w_out.shape[0]
        H = (w_uq.shape[1] - nope_total) // RD
        NOPE, VD = nope_total // H, w_out.shape[0] // H
        SEQ = tokens.shape[1]

        def local_block(tok, gin, wdq, gq, wuq, wdkv, gkv, wukv, wo):
            n_prompts = tok.shape[0]
            T = n_prompts * SEQ
            kernel, out_shape, scratch = make_kernel(n_dev, (T, D, QR, KVR, H, NOPE, RD, VD, SEQ))
            me = lax.axis_index('fsdp')
            pack = jnp.zeros((16, math.lcm(D // n_dev, LANES)), BF16)
            for row, g in enumerate((gin, gq, gkv)):
                period = math.lcm(g.shape[0], LANES) // g.shape[0]
                pack = lax.dynamic_update_slice(pack, g[None, :], (row, lax.rem(me, period) * g.shape[0]))
            wdkv2 = jnp.concatenate([wdkv] + [wdkv[:, KVR:]] * (LANES // RD - 1), axis=1)
            tables = rope_tables(SEQ, RD)
            cmask = np.tril(np.ones((SEQ, SEQ), np.float32))
            lmask = np.zeros((LANES // RD, 1, LANES), np.float32)
            for j in range(LANES // RD):
                lmask[j, 0, j * RD:(j + 1) * RD] = 1
            hbm = pl.BlockSpec(memory_space=pltpu.HBM)
            vmem = pl.BlockSpec(memory_space=pltpu.VMEM)
            outs = pl.pallas_call(
                kernel,
                name="mla",
                out_shape=out_shape,
                in_specs=[hbm] * 7 + [vmem] * 5,
                out_specs=[hbm] * len(out_shape),
                scratch_shapes=scratch,
                compiler_params=pltpu.CompilerParams(collective_id=0, has_side_effects=True, vmem_limit_bytes=67043328),
            )(tok.reshape(T, D), pack, wdkv2, wdq, wuq, wukv, wo,
              *[jnp.asarray(t) for t in tables], jnp.asarray(cmask), jnp.asarray(lmask, BF16))
            rows = lambda n: pl.BlockSpec((SEQ, n), lambda i: (i, 0))
            y, lat, kpe = pl.pallas_call(
                hand_over,
                name="hand_over",
                grid=(n_prompts,),
                out_shape=[jax.ShapeDtypeStruct((T, n), BF16) for n in (D, KVR, RD)],
                in_specs=[rows(D), rows(KVR), rows(LANES)],
                out_specs=[rows(D), rows(KVR), rows(RD)],
            )(*outs[:3])
            return y.reshape(tok.shape), lat.reshape(n_prompts, SEQ, KVR), kpe.reshape(n_prompts, SEQ, RD)

        mapped = jax.shard_map(
            local_block,
            mesh=mesh,
            in_specs=(batch_spec, row_spec, mat_spec, row_spec, mat_spec, mat_spec, row_spec, mat_spec, mat_spec),
            out_specs=(batch_spec, batch_spec, batch_spec),
            check_vma=False,
        )
        return mapped(tokens, gain_in, w_dq, gain_q, w_uq, w_dkv, gain_kv, w_ukv, w_out)

    return run_block
```

time: 811 us -> 603 us (0.74)
  Pallas kernels: 0 us -> 584 us
  matrix products: 338 us -> 0 us
  waiting for transfers between devices: 328 us -> 0 us
  blocking collectives: 51.4 us -> 0 us
  local copies, waits for them, and re-layouts: 52.1 us -> 8.22 us
  other arithmetic: 19.2 us -> 1.76 us
  between operations: 14.4 us -> 1.1 us
    pallas_call x0 -> x2, Pallas kernels: none -> 584 us  [the longest x1 571 us: local_block(): pl.pallas_call(kernel, name='mla', out_shape=out_shape, in_specs=[hbm] *...]
    all_gather x5 -> x0, waiting for transfers between devices: 325 us -> none  [the longest x1 185 us: local_block(): w_out_all = lax.all_gather(w_out_s, 'fsdp', tiled=True)]
    dot_general x7 -> x0, matrix products: 294 us -> none  [the longest x1 134 us: attend(): jnp.einsum('btc,cd->btd', attn_out, w_out, preferred_element_type=jnp.flo...]
    unnamed x1 -> x0, blocking collectives: 51.4 us -> none
    sub x1 -> x0, matrix products: 44 us -> none  [attend(): attn_probs = jax.nn.softmax(scores, axis=-1).astype(jnp.bfloat16)]
    unnamed x20 -> x1, local copies, waits for them, and re-layouts: 26.9 us -> 1.73 us
    slice x1, local copies, waits for them, and re-layouts: 25.2 us -> 0.82 us  [local_block(): wdkv[:, KVR:]]
    another operation x2 -> x0, other arithmetic: 9.23 us -> none  [run_block(): mapped(tokens, gain_in, w_dq, gain_q, w_uq, w_dkv, gain_kv, w_ukv, w_out)]
  transfers between devices with their start and end apart: 5 -> 0, of which waited for: 4 -> 0; matrix products, arithmetic and copies ran while one was open for 34% -> 0% of each run, Pallas kernels for 0% -> 0%
where the time goes in v1:
time: 603 us; the launch traced here: 595 us
  Pallas kernels  584 us (97%)
  local copies, waits for them, and re-layouts  8.22 us (1%)
    pallas_call x1, Pallas kernels, local_block(): pl.pallas_call(kernel, name='mla', out_shape=out_shape, in_specs=[hbm] *...  571 us
    pallas_call x1, Pallas kernels, local_block(): pl.pallas_call(hand_over, name='hand_over', grid=(n_prompts,), out_shape=...  13.3 us

profile of v1, /device:TPU:97, one launch (start us, length us, event | category | flops | bytes accessed | tf_op | source)
XLA Modules:
  0.0 594.9 jit_solution(2161396070400067913)
XLA Ops:
  0.7 0.7 broadcast_in_dim.13
  1.3 0.6 broadcast_in_dim.12
  1.9 1.5 dynamic_update_slice.9
  3.4 1.5 dynamic_update_slice.10
  4.9 1.5 dynamic_update_slice.11.gp
  6.3 0.8 slice.3
  7.1 1.8 pad_maximum_fusion.wdkv
  8.9 570.5 %mla.1 = (bf16[1024,7168]{1,0:T(8,128)(2,1)}, bf16[1024,512]{1,0:T(8,128)(2,1)}, bf16[1024,128]{1,0:T(8,128)(2,1)}, bf16[4,4,2,16,896]{4,3,2,1,0:T(8,128)(2,1)},...) custom-call(bf16[1024,7168]{1,0:T(8,128)(2,1)} %bitcast.6, ...), custom_call_target="tpu_custom_call" | custom-call | tf_op jit(solution)/shard_map/mla/pallas_call | solution.py:493
  579.4 13.3 %hand_over.1 = (bf16[1024,7168]{1,0:T(8,128)(2,1)}, bf16[1024,512]{1,0:T(8,128)(2,1)}, bf16[1024,64]{1,0:T(8,128)(2,1)}) custom-call(bf16[1024,7168]{1,0:T(8,128)(2,1)} %get-tuple-element.9.y_ref, bf16[1024,512]{1,0:T(8,128)(2,1)} %get-tuple-element.10.lat_ref, bf16[1024,128]{1,0:T(8,128)(2,1)} %get-tuple-element.11.kpe_ref), custom_call_target="tpu_custom_call" | custom-call | tf_op jit(solution)/shard_map/hand_over/pallas_call | solution.py:504
  592.8 1.7 copy.17
